TPU v7x, 32 devices: a whole 2x2x4 slice. The times are simulated.
32 devices in a mesh: gx: 8 (over z, y), gy: 4 (over x, core).
Axes of the slice: x: 2, y: 2, z: 4, core: 2. Of those that a mesh axis runs over, the one named last changes fastest.
Arguments:
- rhs: bfloat16 [512, 32768], P(None, ('gy', 'gx')), may hold values from -6 to 6
- leaf_inverse: bfloat16 [32, 1024, 1024], P(('gy', 'gx')), may hold values from -0.1875 to 0.1875
- up_basis: bfloat16 [5, 128, 32768], P(None, None, ('gy', 'gx')), may hold values from -0.25 to 0.25
- projection: bfloat16 [5, 256, 32768], P(None, None, ('gy', 'gx')), may hold values from -0.13258252 to 0.13258252, as said below
Outputs:
- solution: float32 [512, 32768], P(None, ('gy', 'gx'))
Inputs may be any that keep to these rules, and one draw needn't show every extreme that they name: `projection`: rows of level h (counted from 1) have entries of order (2^h * 1024)^(-1/2).
All inputs are finite; a program needn't handle non-finite values.
Results may differ from a plain program's by a relative error of at most 0.0095.
Values sent between devices are 32-bit elements; how exact they have to be, the bound alone decides.
A program may use at most 64 MiB of HBM per device.

v0:
```python
import functools

import jax
import jax.numpy as jnp
from jax import lax
from jax.experimental import pallas as pl
from jax.experimental.pallas import tpu as pltpu
from jax.sharding import PartitionSpec as P

CHUNKS = 2
SUBLANES = 8
TILE = 1024
F32 = jnp.float32
BF16 = jnp.bfloat16


def level_plan(height, bits_x, rows):
    top = height - 1
    groups = []
    low = [b for b in range(min(top, bits_x))]
    high = [b for b in range(bits_x, top)]
    if top == bits_x:
        groups.append([top])
    elif top > bits_x:
        groups.append([bits_x])
        last = [top] + high[1:]
        if len(low) <= 3 and rows >> len(low) + len(high) >= SUBLANES:
            last, low = last + low, []
        groups.append(last)
    if top < bits_x and len(low) < 3:
        groups.append(low + [top])
    else:
        while low:
            groups.append(low[:3])
            low = low[3:]
        if top < bits_x:
            groups.append([top])
    phases = []
    for bits in groups:
        split = [b for b in bits if b != top]
        if rows >> len(split) < SUBLANES:
            assert top not in bits
            phases.append(("sum", bits))
        else:
            rows >>= len(split)
            phases.append(("scatter", bits))
    return phases


def masks_of(bits):
    masks = [0]
    for b in bits:
        masks += [m | 1 << b for m in masks]
    return masks[1:]


def sub_index(pos, bits):
    index = 0
    for k, b in enumerate(bits):
        index = index + ((pos >> b) & 1) * (1 << k)
    return index


def build_plan(levels, bits_x, rows, rank):
    plan, shapes, sems = [], [], 0

    def buf(*shape):
        shapes.append(shape)
        return len(shapes) - 1

    for height in range(1, levels + 1):
        top = height - 1
        n, c = rows, 2
        source = buf(c, n, rank)
        steps = []
        for kind, bits in level_plan(height, bits_x, rows):
            masks = masks_of(bits)
            split = [b for b in bits if b != top] if kind == "scatter" else []
            n >>= len(split)
            if top in bits:
                c = 1
            landing = buf(len(masks), c, n, rank)
            result = buf(c, n, rank)
            steps.append((kind, bits, split, masks, source, landing, result, n, c, sems))
            sems += len(masks)
            source = result
        for _, bits, split, *_ in reversed(list(steps)):
            if not split:
                continue
            masks = masks_of(split)
            result = buf(1, n << len(split), rank)
            steps.append(("gather", split, split, masks, source, None, result, n, 1, sems))
            sems += len(masks)
            n <<= len(split)
            source = result
        plan.append(steps)
    return plan, shapes, sems


def kernel(dims, plan, rhs_hbm, leaf_hbm, up_hbm, proj_hbm, out_hbm, last_ref, *scratch):
    bits_x, bits_y, levels, chunks, rows, points, rank = dims
    rhs, leaf, up, proj, state, rounded = scratch[:6]
    in_sems, out_sems, send_sems, recv_sems = scratch[6:10]
    per_chunk = (len(scratch) - 10) // chunks
    gx, gy = lax.axis_index("gx"), lax.axis_index("gy")
    pos = gy * (1 << bits_x) + gx

    def device(mask):
        return {"gx": gx ^ (mask & ((1 << bits_x) - 1)), "gy": gy ^ (mask >> bits_x)}

    loads = [
        pltpu.make_async_copy(rhs_hbm, rhs, in_sems.at[0]),
        pltpu.make_async_copy(leaf_hbm.at[0], leaf, in_sems.at[1]),
    ]
    for level in range(levels):
        loads.append(pltpu.make_async_copy(proj_hbm.at[level], proj.at[level], in_sems.at[2 + 2 * level]))
        if level < levels - 1:
            loads.append(pltpu.make_async_copy(up_hbm.at[level], up.at[level], in_sems.at[3 + 2 * level]))
    for load in loads:
        load.start()

    everyone = set()
    for steps in plan:
        for step in steps:
            everyone.update(step[3])
    barrier = pltpu.get_barrier_semaphore()
    for mask in sorted(everyone):
        pl.semaphore_signal(barrier, inc=1, device_id=device(mask), device_id_type=pl.DeviceIdType.MESH)
    loads[0].wait()
    loads[1].wait()

    def leaf_apply(lo):
        @pl.loop(0, points // TILE)
        def _(tile):
            cols = pl.ds(pl.multiple_of(tile * TILE, TILE), TILE)
            value = jnp.dot(rhs[lo : lo + rows, :], leaf[:, cols], preferred_element_type=F32)
            state[lo : lo + rows, cols] = value
            rounded[lo : lo + rows, cols] = value.astype(BF16)

    def update(lo, level, coefficient):
        @pl.loop(0, points // TILE)
        def _(tile):
            cols = pl.ds(pl.multiple_of(tile * TILE, TILE), TILE)
            value = state[lo : lo + rows, cols] - jnp.dot(
                coefficient, up[level, :, cols], preferred_element_type=F32
            )
            state[lo : lo + rows, cols] = value
            rounded[lo : lo + rows, cols] = value.astype(BF16)

    leaf_apply(0)
    pl.semaphore_wait(barrier, len(everyone))

    def flow(chunk):
        lo = chunk * rows
        bufs = scratch[10 + chunk * per_chunk : 10 + (chunk + 1) * per_chunk]
        if chunk:
            leaf_apply(lo)
        sends = []
        for level in range(levels):
            top = level
            if chunk == 0:
                loads[2 + 2 * level].wait()
            whole = bufs[plan[level][0][4]]
            for half in range(2):
                whole[half] = lax.dot_general(
                    rounded[lo : lo + rows, :],
                    proj[level, half * rank : (half + 1) * rank, :],
                    (((1,), (1,)), ((), ())),
                    preferred_element_type=F32,
                )
            bit = (pos >> top) & 1
            for kind, bits, split, masks, src, landing, dst, n, c, sem in plan[level]:
                copies = []
                src_ref, dst_ref = bufs[src], bufs[dst]

                def piece(who):
                    row = pl.ds(pl.multiple_of(sub_index(who, split) * n, n), n)
                    if top in bits:
                        return pl.ds((who >> top) & 1, 1), row
                    return pl.ds(0, c), row

                if kind == "gather":
                    own = pl.ds(pl.multiple_of(sub_index(pos, split) * n, n), n)
                for k, mask in enumerate(masks):
                    if kind == "gather":
                        frm, to = src_ref, dst_ref.at[:, own]
                    else:
                        frm, to = src_ref.at[piece(pos ^ mask)], bufs[landing].at[k]
                    copy = pltpu.make_async_remote_copy(
                        src_ref=frm,
                        dst_ref=to,
                        send_sem=send_sems.at[chunk, sem + k],
                        recv_sem=recv_sems.at[chunk, sem + k],
                        device_id=device(mask),
                        device_id_type=pl.DeviceIdType.MESH,
                    )
                    copy.start()
                    copies.append(copy)
                sends += copies
                if kind == "gather":
                    dst_ref[:, own] = src_ref[...]
                yield
                if kind == "gather":
                    for copy in copies:
                        copy.wait_recv()
                else:
                    for copy in copies:
                        copy.wait_recv()
                    total = src_ref[piece(pos)]
                    for k in range(len(masks)):
                        total = total + bufs[landing][k]
                    dst_ref[...] = total
            coefficient = bufs[plan[level][-1][6]][0].astype(BF16)
            if level == levels - 1:
                last_ref[lo : lo + rows, :] = coefficient
                break
            if chunk == 0:
                loads[3 + 2 * level].wait()
            update(lo, level, coefficient)
            if level == levels - 2:
                store = pltpu.make_async_copy(
                    state.at[lo : lo + rows], out_hbm.at[lo : lo + rows], out_sems.at[chunk]
                )
                store.start()
        for copy in sends:
            copy.wait_send()
        yield
        store.wait()

    flows = [flow(chunk) for chunk in range(chunks)]
    while flows:
        left = []
        for item in flows:
            try:
                next(item)
                left.append(item)
            except StopIteration:
                pass
        flows = left


def shards(rhs, leaf_inverse, up_basis, projection):
    bits_x = lax.axis_size("gx").bit_length() - 1
    bits_y = lax.axis_size("gy").bit_length() - 1
    levels, rank, points = up_basis.shape
    rows = rhs.shape[0] // CHUNKS
    plan, shapes, sems = build_plan(levels, bits_x, rows, rank)
    dims = (bits_x, bits_y, levels, CHUNKS, rows, points, rank)
    any_spec = pl.BlockSpec(memory_space=pl.ANY)
    state, coefficient = pl.pallas_call(
        functools.partial(kernel, dims, plan),
        out_shape=(
            jax.ShapeDtypeStruct(rhs.shape, F32),
            jax.ShapeDtypeStruct((rhs.shape[0], rank), BF16),
        ),
        in_specs=[any_spec] * 4,
        out_specs=(any_spec, pl.BlockSpec(memory_space=pltpu.VMEM)),
        scratch_shapes=[
            pltpu.VMEM(rhs.shape, BF16),
            pltpu.VMEM(leaf_inverse.shape[1:], BF16),
            pltpu.VMEM(up_basis.shape, BF16),
            pltpu.VMEM(projection.shape, BF16),
            pltpu.VMEM(rhs.shape, F32),
            pltpu.VMEM(rhs.shape, BF16),
            pltpu.SemaphoreType.DMA((2 + 2 * levels,)),
            pltpu.SemaphoreType.DMA((CHUNKS,)),
            pltpu.SemaphoreType.DMA((CHUNKS, sems)),
            pltpu.SemaphoreType.DMA((CHUNKS, sems)),
        ]
        + [pltpu.VMEM(shape, F32) for _ in range(CHUNKS) for shape in shapes],
        compiler_params=pltpu.CompilerParams(
            collective_id=0, has_side_effects=True, vmem_limit_bytes=60 * 2**20
        ),
    )(rhs, leaf_inverse, up_basis, projection)
    return state - jnp.dot(coefficient, up_basis[levels - 1], preferred_element_type=F32)


def solution(mesh):
    return jax.shard_map(
        shards,
        mesh=mesh,
        in_specs=(
            P(None, ("gy", "gx")),
            P(("gy", "gx"), None, None),
            P(None, None, ("gy", "gx")),
            P(None, None, ("gy", "gx")),
        ),
        out_specs=P(None, ("gy", "gx")),
        check_vma=False,
    )
```

profile of v0, /device:TPU:0, one launch (start us, length us, event | category | flops | bytes accessed | tf_op | source)
XLA Modules:
  0.0 73.1 jit_solution(16269928456249662373)
XLA Ops:
  0.0 69.6 %shard_map.46 = (f32[512,1024]{1,0:T(8,128)}, bf16[512,128]{1,0:T(8,128)(2,1)}) custom-call(bf16[512,1024]{1,0:T(8,128)(2,1)} %rhs_hbm.1, bf16[1,1024,1024]{2,1,0:T(8,128)(2,1)} %leaf_hbm.1, bf16[5,128,1024]{2,1,0:T(8,128)(2,1)} %up_hbm.1, bf16[5,256,1024]{2,1,0:T(8,128)(2,1)} %proj_hbm.1), custom_call_target="tpu_custom_call" | custom-call | tf_op jit(solution)/shard_map/pallas_call | solution.py:250
  69.6 3.5 %convolution_subtract_fusion = f32[512,1024]{1,0:T(8,128)} fusion(f32[512,1024]{1,0:T(8,128)} %get-tuple-element.7, bf16[512,128]{1,0:T(8,128)(2,1)} %get-tuple-element.8, bf16[5,128,1024]{2,1,0:T(8,128)(2,1)} %up_hbm.1), kind=kOutput, calls=%fused_computation | convolution fusion | flops 134742016 | bytes 4587520 | tf_op jit(solution)/shard_map/dot_general | solution.py:275
where the time goes:
time: 73.3 us; the launch traced here: 73.1 us
  Pallas kernels  69.6 us (95%)
  matrix products  3.51 us (5%)
    pallas_call x1, Pallas kernels, shards(): pl.pallas_call(functools.partial(kernel, dims, plan), out_shape=(jax.Shap...  69.6 us
    dot_general x1, matrix products, shards(): jnp.dot(coefficient, up_basis[levels - 1], preferred_element_type=F32)  3.51 us

commit v1 on v0

v1 whole, which is shorter than its diff:
```python
import functools

import jax
import jax.numpy as jnp
from jax import lax
from jax.experimental import pallas as pl
from jax.experimental.pallas import tpu as pltpu
from jax.sharding import PartitionSpec as P

CHUNKS = 2
SUBLANES = 8
F32 = jnp.float32
BF16 = jnp.bfloat16
MESH = pl.DeviceIdType.MESH


def level_plan(height, bits_x, rows):
    top = height - 1
    groups = []
    low = [b for b in range(min(top, bits_x))]
    high = [b for b in range(bits_x, top)]
    if top == bits_x:
        groups.append([top])
    elif top > bits_x:
        groups.append([bits_x])
        last = [top] + high[1:]
        if len(low) <= 3 and rows >> len(low) + len(high) >= SUBLANES:
            last, low = last + low, []
        groups.append(last)
    if top < bits_x and len(low) < 3:
        groups.append(low + [top])
    else:
        while low:
            groups.append(low[:3])
            low = low[3:]
        if top < bits_x:
            groups.append([top])
    phases = []
    for bits in groups:
        split = [b for b in bits if b != top]
        if rows >> len(split) < SUBLANES:
            assert top not in bits
            phases.append((bits, []))
        else:
            rows >>= len(split)
            phases.append((bits, split))
    return phases


def masks_of(bits):
    masks = [0]
    for b in bits:
        masks += [m | 1 << b for m in masks]
    return masks[1:]


def triples(bits):
    return [bits[i : i + 3] for i in range(0, len(bits), 3)]


def sub_index(pos, bits):
    index = 0
    for k, b in enumerate(bits):
        index = index + ((pos >> b) & 1) * (1 << k)
    return index


class Step:
    def __init__(self, kind, bits, half, block, split, src, landing, dst, shape, sem):
        self.kind, self.masks = kind, masks_of(bits)
        self.half, self.block, self.split = half, block, split
        self.src, self.landing, self.dst = src, landing, dst
        self.shape, self.sem = shape, sem


class Buffers:
    def __init__(self):
        self.shapes, self.sems = [], 0

    def new(self, *shape):
        self.shapes.append(shape)
        return len(self.shapes) - 1

    def reduce(self, src, shape, bits, half=None, block=None, split=()):
        c, b, n, r = shape
        shape = (1 if half is not None else c, 1 if block is not None else b, n >> len(split), r)
        landing = self.new(2 ** len(bits) - 1, *shape)
        step = Step("reduce", bits, half, block, list(split), src, landing, self.new(*shape), shape, self.sems)
        self.sems += len(step.masks)
        return step

    def gather(self, src, shape, split, block=None):
        c, b, n, r = shape
        bits = list(split) + ([] if block is None else [block])
        whole = (c, b if block is None else 2, n << len(split), r)
        step = Step("gather", bits, None, block, list(split), src, None, self.new(*whole), shape, self.sems)
        self.sems += len(step.masks)
        return step

    def chain(self, src, shape, makers):
        steps = []
        for make in makers:
            steps.append(make(src, shape))
            src, shape = steps[-1].dst, self.shapes[steps[-1].dst]
        return steps, src, shape


def group_levels(levels, rows):
    groups, height = [], 1
    while height <= levels:
        pair = height % 2 == 0 and height < levels and rows // 2 >> height - 1 >= SUBLANES
        groups.append((height, height + 1) if pair else (height,))
        height += len(groups[-1])
    return groups


def build_plan(levels, bits_x, rows, rank):
    plan, space, tables = [], Buffers(), {}
    for group in group_levels(levels, rows):
        height = group[0]
        top = height - 1
        entry = {"group": group}
        if len(group) == 1:
            shape = (2, 1, rows, rank)
            tables[height] = space.new(*shape)
            makers, splits = [], []
            for bits, split in level_plan(height, bits_x, rows):
                half = top if top in bits else None
                makers.append(functools.partial(space.reduce, bits=bits, half=half, split=split))
                if split:
                    splits.append(split)
            entry["reduce"], src, shape = space.chain(tables[height], shape, makers)
            makers = [functools.partial(space.gather, split=s) for s in reversed(splits)]
            entry["gather"], entry["result"], _ = space.chain(src, shape, makers)
        else:
            low = list(range(top))
            shape = (2, 2, rows // 2, rank)
            first, second = space.new(*shape), space.new(*shape)
            tables[height], tables[height + 1] = first, second
            parts = [functools.partial(space.reduce, bits=g, split=g) for g in triples(low)]
            own = functools.partial(space.reduce, bits=[top], half=top)
            entry["early"] = top == bits_x
            if entry["early"]:
                one = [own] + parts
                two = [functools.partial(space.reduce, bits=[top], block=top)] + parts
            elif len(low) < 3:
                one = [functools.partial(space.reduce, bits=low + [top], half=top, split=low)]
                two = parts
            else:
                one, two = parts + [own], parts
            entry["one"], src, shape = space.chain(first, shape, one)
            entry["owned"], n = src, shape[2]
            makers = [functools.partial(space.gather, split=g) for g in reversed(triples(low))]
            entry["gather_one"], entry["result_one"], _ = space.chain(src, shape, makers)
            entry["two"], entry["partial"], _ = space.chain(second, (2, 2, rows // 2, rank), two)
            shape = (2, 2, n, rank)
            entry["joined"] = space.new(*shape)
            entry["last"] = space.reduce(entry["joined"], shape, [top, height], half=height, block=top)
            shape = entry["last"].shape
            if len(low) <= 3:
                makers = [functools.partial(space.gather, split=low, block=top)]
            else:
                makers = [functools.partial(space.gather, split=[], block=top)]
                makers += [functools.partial(space.gather, split=g) for g in reversed(triples(low))]
            entry["gather_two"], entry["result_two"], _ = space.chain(entry["last"].dst, shape, makers)
        plan.append(entry)
    return plan, space, tables


def build_sums(plan, rank):
    space, sums = Buffers(), []
    for entry in plan:
        if len(entry["group"]) == 1:
            continue
        height = entry["group"][0]
        low = list(range(height - 1))
        shape = (2, 1, rank, rank)
        src = space.new(*shape)
        makers, splits, n = [], [], rank
        for g in triples(low):
            split = g if len(low) > 1 and n >> len(g) >= SUBLANES else []
            n >>= len(split)
            makers.append(functools.partial(space.reduce, bits=g, split=split))
            if split:
                splits.append(split)
        steps, dst, shape = space.chain(src, shape, makers)
        makers = [functools.partial(space.gather, split=s) for s in reversed(splits)]
        more, dst, _ = space.chain(dst, shape, makers)
        sums.append((height, src, steps + more, dst))
    return sums, space


def kernel(dims, plan, tables, sums, counts, rhs_hbm, leaf_hbm, up_hbm, proj_hbm, state, last_ref, *scratch):
    bits_x, bits_y, levels, chunks, rows, rank = dims
    rhs, leaf, up, proj, rounded, coef, mix, mix_sum = scratch[:8]
    in_sems, send_sems, recv_sems, sum_send, sum_recv = scratch[8:13]
    per_chunk = counts[0]
    gx, gy = lax.axis_index("gx"), lax.axis_index("gy")
    pos = gy * (1 << bits_x) + gx

    def device(mask):
        return {"gx": gx ^ (mask & ((1 << bits_x) - 1)), "gy": gy ^ (mask >> bits_x)}

    loads = {
        "rhs": pltpu.make_async_copy(rhs_hbm, rhs, in_sems.at[0]),
        "leaf": pltpu.make_async_copy(leaf_hbm.at[0], leaf, in_sems.at[1]),
    }
    for level in range(levels):
        loads["proj", level] = pltpu.make_async_copy(proj_hbm.at[level], proj.at[level], in_sems.at[2 + 2 * level])
        if level < levels - 1:
            loads["up", level] = pltpu.make_async_copy(up_hbm.at[level], up.at[level], in_sems.at[3 + 2 * level])
    for load in loads.values():
        load.start()

    def need(*key):
        load = loads.pop(key if len(key) > 1 else key[0], None)
        if load is not None:
            load.wait()

    greeted = {1 << b for b in range(bits_x + bits_y)}
    for entry in plan:
        group = entry["group"]
        if len(group) == 1:
            for step in entry["reduce"] + entry["gather"]:
                greeted.update(step.masks)
        elif group[0] == bits_x + 1:
            greeted.update(entry["last"].masks)
        else:
            for step in entry["one"]:
                greeted.update(step.masks)
    barrier = pltpu.get_barrier_semaphore()
    for mask in sorted(greeted):
        pl.semaphore_signal(barrier, inc=1, device_id=device(mask), device_id_type=MESH)

    sent = []

    def start(step, bufs, send, recv):
        src, dst = bufs[step.src], bufs[step.dst]
        n = step.shape[2]

        def piece(who):
            halves = pl.ds(0, step.shape[0]) if step.half is None else pl.ds((who >> step.half) & 1, 1)
            blocks = pl.ds(0, step.shape[1]) if step.block is None else pl.ds((who >> step.block) & 1, 1)
            return halves, blocks, pl.ds(pl.multiple_of(sub_index(who, step.split) * n, n), n)

        copies = []
        for k, mask in enumerate(step.masks):
            if step.kind == "gather":
                frm, to = src, dst.at[piece(pos)]
            else:
                frm, to = src.at[piece(pos ^ mask)], bufs[step.landing].at[k]
            copy = pltpu.make_async_remote_copy(
                src_ref=frm,
                dst_ref=to,
                send_sem=send(step.sem + k),
                recv_sem=recv(step.sem + k),
                device_id=device(mask),
                device_id_type=MESH,
            )
            copy.start()
            copies.append(copy)
        sent.extend(copies)
        if step.kind == "gather":
            dst[piece(pos)] = src[...]

        def finish():
            for copy in copies:
                copy.wait_recv()
            if step.kind == "reduce":
                total = src[piece(pos)]
                for k in range(len(step.masks)):
                    total = total + bufs[step.landing][k]
                dst[...] = total

        return finish

    def mixing(low, high):
        return low * levels + high

    def flow(chunk):
        lo = chunk * rows
        bufs = scratch[13 + chunk * per_chunk : 13 + (chunk + 1) * per_chunk]
        span = slice(lo, lo + rows)

        def begin(step):
            return start(step, bufs, lambda k: send_sems.at[chunk, k], lambda k: recv_sems.at[chunk, k])

        def project(height):
            need("proj", height - 1)
            table = bufs[tables[height]]
            for half in range(2):
                value = lax.dot_general(
                    rounded[span, :],
                    proj[height - 1, half * rank : (half + 1) * rank, :],
                    (((1,), (1,)), ((), ())),
                    preferred_element_type=F32,
                )
                table[half] = value.reshape(table.shape[1:])

        def keep(height, ref):
            value = ref[0].reshape(rows, rank).astype(BF16)
            if height == levels:
                last_ref[span, :] = value
            else:
                coef[height - 1, span, :] = value

        def correct(done, heights):
            for height in heights:
                delta = jnp.dot(coef[done - 1, span, :], mix[mixing(done, height)], preferred_element_type=F32)
                table = bufs[tables[height]]
                for half in range(2):
                    part = delta[:, half * rank : (half + 1) * rank]
                    table[half] = table[half] - part.reshape(table.shape[1:])

        def update(heights):
            value = state[span, :]
            for height in heights:
                need("up", height - 1)
                value = value - jnp.dot(coef[height - 1, span, :], up[height - 1], preferred_element_type=F32)
            state[span, :] = value

        need("rhs")
        need("leaf")
        value = jnp.dot(rhs[span, :], leaf[...], preferred_element_type=F32)
        state[span, :] = value
        rounded[span, :] = value.astype(BF16)
        project(1)
        if chunk == 0:
            pl.semaphore_wait(barrier, len(greeted))

        later = []
        for index, entry in enumerate(plan):
            group = entry["group"]
            after = [h for e in plan[index + 1 : index + 2] for h in e["group"]]
            beyond = [h for e in plan[index + 2 :] for h in e["group"]]
            if len(group) == 1:
                height = group[0]
                for step in entry["reduce"] + entry["gather"]:
                    finish = begin(step)
                    for work in later:
                        work()
                    later = []
                    yield
                    if height == 1 and step is entry["reduce"][0]:
                        for other in range(2, levels + 1):
                            project(other)
                    finish()
                keep(height, bufs[entry["result"]])
                if height < levels:
                    correct(height, after)
                    later = [functools.partial(correct, height, beyond), functools.partial(update, [height])]
            else:
                height = group[0]
                one, two = entry["one"], entry["two"]
                first, second = begin(one[0]), begin(two[0])
                for work in later:
                    work()
                later = []
                for i in range(max(len(one), len(two))):
                    yield
                    if i < len(one):
                        first()
                        if i + 1 < len(one):
                            first = begin(one[i + 1])
                        else:
                            fetch = begin(entry["gather_one"][0])
                    if i < len(two):
                        second()
                        if i + 1 < len(two):
                            second = begin(two[i + 1])
                owned, joined, base = bufs[entry["owned"]], bufs[entry["joined"]], bufs[entry["partial"]]
                n = owned.shape[2]
                complete(height)
                table = mix_sum[[s[0] for s in sums].index(height)]
                delta = jnp.dot(owned[0].reshape(2 * n, rank).astype(BF16), table, preferred_element_type=F32)
                for half in range(2):
                    for block in range(2):
                        part = delta[block * n : (block + 1) * n, half * rank : (half + 1) * rank]
                        if entry["early"]:
                            mine = ((pos >> height - 1) & 1) == block
                            joined[half, block] = jnp.where(mine, base[half, 0], 0.0) - part
                        else:
                            joined[half, block] = base[half, block] - part
                finish = begin(entry["last"])
                yield
                finish()
                finish = begin(entry["gather_two"][0])
                fetch()
                for step in entry["gather_one"][1:]:
                    fetch = begin(step)
                    yield
                    fetch()
                keep(height, bufs[entry["result_one"]])
                correct(height, after)
                later = [functools.partial(correct, height, beyond)]
                if after:
                    later.append(functools.partial(correct, height + 1, beyond))
                    later.append(functools.partial(update, [height, height + 1]))
                else:
                    update([height])
                    later = []
                yield
                finish()
                for step in entry["gather_two"][1:]:
                    finish = begin(step)
                    yield
                    finish()
                keep(height + 1, bufs[entry["result_two"]])
                if after:
                    correct(height + 1, after)

    sum_bufs = scratch[13 + chunks * per_chunk :]
    running = {}

    def compute(low, high):
        need("up", low - 1)
        need("proj", high - 1)
        value = lax.dot_general(up[low - 1], proj[high - 1], (((1,), (1,)), ((), ())), preferred_element_type=F32)
        mix[mixing(low, high)] = value.astype(BF16)
        return value

    def advance(height):
        for k, (key, src, steps, dst) in enumerate(sums):
            if key != height:
                continue
            if height in running:
                at, finish = running[height]
                if finish is None:
                    return
                finish()
            else:
                at = -1
            at += 1
            if at < len(steps):
                begun = start(steps[at], sum_bufs, lambda i: sum_send.at[i], lambda i: sum_recv.at[i])
                running[height] = (at, begun)
            else:
                running[height] = (at, None)
                for half in range(2):
                    mix_sum[k, :, half * rank : (half + 1) * rank] = sum_bufs[dst][half, 0].astype(BF16)

    def complete(height):
        while running.get(height, (0, 0))[1] is not None:
            advance(height)

    def summing():
        for low in range(1, levels):
            for high in range(low + 1, levels + 1):
                value = compute(low, high)
                for height, src, _, _ in sums:
                    if (low, high) == (height, height + 1):
                        for half in range(2):
                            sum_bufs[src][half, 0] = value[:, half * rank : (half + 1) * rank]
        order = [entry[0] for entry in sums]
        for height in order:
            advance(height)
            yield
            advance(height)
            yield
            if height != order[0]:
                complete(height)

    flows = [flow(chunk) for chunk in range(chunks)] + [summing()]
    while flows:
        left = []
        for item in flows:
            try:
                next(item)
                left.append(item)
            except StopIteration:
                pass
        flows = left
    for copy in sent:
        copy.wait_send()
    for key in list(loads):
        loads.pop(key).wait()


def shards(rhs, leaf_inverse, up_basis, projection):
    bits_x = lax.axis_size("gx").bit_length() - 1
    bits_y = lax.axis_size("gy").bit_length() - 1
    levels, rank, points = up_basis.shape
    rows = rhs.shape[0] // CHUNKS
    plan, space, tables = build_plan(levels, bits_x, rows, rank)
    sums, more = build_sums(plan, rank)
    dims = (bits_x, bits_y, levels, CHUNKS, rows, rank)
    hbm_spec = pl.BlockSpec(memory_space=pltpu.MemorySpace.HBM)
    vmem_spec = pl.BlockSpec(memory_space=pltpu.VMEM)
    state, coefficient = pl.pallas_call(
        functools.partial(kernel, dims, plan, tables, sums, (len(space.shapes),)),
        out_shape=(
            jax.ShapeDtypeStruct((rhs.shape[0], points), F32),
            jax.ShapeDtypeStruct((rhs.shape[0], rank), BF16),
        ),
        in_specs=[hbm_spec] * 4,
        out_specs=(vmem_spec, vmem_spec),
        scratch_shapes=[
            pltpu.VMEM(rhs.shape, BF16),
            pltpu.VMEM(leaf_inverse.shape[1:], BF16),
            pltpu.VMEM(up_basis.shape, BF16),
            pltpu.VMEM(projection.shape, BF16),
            pltpu.VMEM((rhs.shape[0], points), BF16),
            pltpu.VMEM((levels - 1, rhs.shape[0], rank), BF16),
            pltpu.VMEM((levels * (levels + 1), rank, 2 * rank), BF16),
            pltpu.VMEM((max(len(sums), 1), rank, 2 * rank), BF16),
            pltpu.SemaphoreType.DMA((2 + 2 * levels,)),
            pltpu.SemaphoreType.DMA((CHUNKS, space.sems)),
            pltpu.SemaphoreType.DMA((CHUNKS, space.sems)),
            pltpu.SemaphoreType.DMA((max(more.sems, 1),)),
            pltpu.SemaphoreType.DMA((max(more.sems, 1),)),
        ]
        + [pltpu.VMEM(shape, F32) for _ in range(CHUNKS) for shape in space.shapes]
        + [pltpu.VMEM(shape, F32) for shape in more.shapes],
        compiler_params=pltpu.CompilerParams(
            collective_id=0, has_side_effects=True, vmem_limit_bytes=44 * 2**20
        ),
    )(*[pltpu.with_memory_space_constraint(x, pltpu.MemorySpace.HBM) for x in (rhs, leaf_inverse, up_basis, projection)])
    return state - jnp.dot(coefficient, up_basis[levels - 1], preferred_element_type=F32)


def solution(mesh):
    return jax.shard_map(
        shards,
        mesh=mesh,
        in_specs=(
            P(None, ("gy", "gx")),
            P(("gy", "gx"), None, None),
            P(None, None, ("gy", "gx")),
            P(None, None, ("gy", "gx")),
        ),
        out_specs=P(None, ("gy", "gx")),
        check_vma=False,
    )
```

time: 73.3 us -> 69.5 us (0.948)
  Pallas kernels: 69.6 us -> 66.7 us
  matrix products: 3.51 us -> 2.7 us
    pallas_call x1, Pallas kernels: 69.6 us -> 66.7 us  [shards(): pl.pallas_call(functools.partial(kernel, dims, plan, tables, sums, (len(s...]
    dot_general x1, matrix products: 3.51 us -> 2.7 us  [shards(): jnp.dot(coefficient, up_basis[levels - 1], preferred_element_type=F32)]
where the time goes in v1:
time: 69.5 us; the launch traced here: 69.4 us
  Pallas kernels  66.7 us (96%)
  matrix products  2.7 us (4%)
    pallas_call x1, Pallas kernels, shards(): pl.pallas_call(functools.partial(kernel, dims, plan, tables, sums, (len(s...  66.7 us
    dot_general x1, matrix products, shards(): jnp.dot(coefficient, up_basis[levels - 1], preferred_element_type=F32)  2.7 us

profile of v1, /device:TPU:0, one launch (start us, length us, event | category | flops | bytes accessed | tf_op | source)
XLA Modules:
  0.0 69.4 jit_solution(6513050424029963861)
XLA Ops:
  0.0 66.7 %shard_map.46 = (f32[512,1024]{1,0:T(8,128)S(1)}, bf16[512,128]{1,0:T(8,128)(2,1)S(1)}) custom-call(bf16[512,1024]{1,0:T(8,128)(2,1)} %rhs_hbm.1, bf16[1,1024,1024]{2,1,0:T(8,128)(2,1)} %leaf_hbm.1, bf16[5,128,1024]{2,1,0:T(8,128)(2,1)} %up_hbm.1, bf16[5,256,1024]{2,1,0:T(8,128)(2,1)} %proj_hbm.1), custom_call_target="tpu_custom_call" | custom-call | tf_op jit(solution)/shard_map/pallas_call | solution.py:489
  66.7 2.7 %convolution_subtract_fusion = f32[512,1024]{1,0:T(8,128)} fusion(f32[512,1024]{1,0:T(8,128)S(1)} %get-tuple-element.7, bf16[512,128]{1,0:T(8,128)(2,1)S(1)} %get-tuple-element.8, bf16[5,128,1024]{2,1,0:T(8,128)(2,1)} %up_hbm.1), kind=kOutput, calls=%fused_computation | convolution fusion | flops 134742016 | bytes 4587520 | tf_op jit(solution)/shard_map/dot_general | solution.py:518

commit v2 on v1

--- a/solution.py
+++ b/solution.py
@@ -58,6 +58,10 @@
     return [bits[i : i + 3] for i in range(0, len(bits), 3)]
 
 
+def pairs(bits):
+    return [bits[i : i + 2] for i in range(0, len(bits), 2)]
+
+
 def sub_index(pos, bits):
     index = 0
     for k, b in enumerate(bits):
@@ -137,31 +141,30 @@
             shape = (2, 2, rows // 2, rank)
             first, second = space.new(*shape), space.new(*shape)
             tables[height], tables[height + 1] = first, second
-            parts = [functools.partial(space.reduce, bits=g, split=g) for g in triples(low)]
+            parts = [functools.partial(space.reduce, bits=g, split=g) for g in pairs(low)]
             own = functools.partial(space.reduce, bits=[top], half=top)
             entry["early"] = top == bits_x
+            one, two = [own] + parts, parts
             if entry["early"]:
-                one = [own] + parts
                 two = [functools.partial(space.reduce, bits=[top], block=top)] + parts
-            elif len(low) < 3:
-                one = [functools.partial(space.reduce, bits=low + [top], half=top, split=low)]
-                two = parts
-            else:
-                one, two = parts + [own], parts
             entry["one"], src, shape = space.chain(first, shape, one)
             entry["owned"], n = src, shape[2]
-            makers = [functools.partial(space.gather, split=g) for g in reversed(triples(low))]
+            makers = [functools.partial(space.gather, split=g) for g in reversed(pairs(low))]
             entry["gather_one"], entry["result_one"], _ = space.chain(src, shape, makers)
             entry["two"], entry["partial"], _ = space.chain(second, (2, 2, rows // 2, rank), two)
             shape = (2, 2, n, rank)
             entry["joined"] = space.new(*shape)
             entry["last"] = space.reduce(entry["joined"], shape, [top, height], half=height, block=top)
             shape = entry["last"].shape
-            if len(low) <= 3:
+            if entry["early"]:
+                nested = [b for g in reversed(pairs(low)) for b in g]
+                makers = [functools.partial(space.gather, split=g) for g in triples(nested)]
+                makers += [functools.partial(space.gather, split=[], block=top)]
+            elif len(low) < 3:
                 makers = [functools.partial(space.gather, split=low, block=top)]
             else:
                 makers = [functools.partial(space.gather, split=[], block=top)]
-                makers += [functools.partial(space.gather, split=g) for g in reversed(triples(low))]
+                makers += [functools.partial(space.gather, split=g) for g in reversed(pairs(low))]
             entry["gather_two"], entry["result_two"], _ = space.chain(entry["last"].dst, shape, makers)
         plan.append(entry)
     return plan, space, tables
@@ -176,13 +179,11 @@
         low = list(range(height - 1))
         shape = (2, 1, rank, rank)
         src = space.new(*shape)
-        makers, splits, n = [], [], rank
-        for g in triples(low):
-            split = g if len(low) > 1 and n >> len(g) >= SUBLANES else []
-            n >>= len(split)
-            makers.append(functools.partial(space.reduce, bits=g, split=split))
-            if split:
-                splits.append(split)
+        makers, splits = [], []
+        for bit in low[1:]:
+            makers.append(functools.partial(space.reduce, bits=[bit], split=[bit]))
+            splits.append([bit])
+        makers.append(functools.partial(space.reduce, bits=low[:1]))
         steps, dst, shape = space.chain(src, shape, makers)
         makers = [functools.partial(space.gather, split=s) for s in reversed(splits)]
         more, dst, _ = space.chain(dst, shape, makers)
@@ -223,7 +224,7 @@
         if len(group) == 1:
             for step in entry["reduce"] + entry["gather"]:
                 greeted.update(step.masks)
-        elif group[0] == bits_x + 1:
+        elif entry["early"]:
             greeted.update(entry["last"].masks)
         else:
             for step in entry["one"]:
@@ -451,14 +452,13 @@
                     if (low, high) == (height, height + 1):
                         for half in range(2):
                             sum_bufs[src][half, 0] = value[:, half * rank : (half + 1) * rank]
-        order = [entry[0] for entry in sums]
-        for height in order:
+        for height, _, _, _ in sums[1:]:
             advance(height)
+        yield
+        for _ in range(max([0] + [len(steps) + 1 for _, _, steps, _ in sums])):
+            for height, _, _, _ in sums:
+                advance(height)
             yield
-            advance(height)
-            yield
-            if height != order[0]:
-                complete(height)
 
     flows = [flow(chunk) for chunk in range(chunks)] + [summing()]
     while flows:

time: 69.5 us -> 61 us (0.88)
  Pallas kernels: 66.7 us -> 58.1 us
    pallas_call x1, Pallas kernels: 66.7 us -> 58.1 us  [shards(): pl.pallas_call(functools.partial(kernel, dims, plan, tables, sums, (len(s...]
where the time goes in v2:
time: 61 us; the launch traced here: 60.8 us
  Pallas kernels  58.1 us (95%)
  matrix products  2.7 us (4%)
    pallas_call x1, Pallas kernels, shards(): pl.pallas_call(functools.partial(kernel, dims, plan, tables, sums, (len(s...  58.1 us
    dot_general x1, matrix products, shards(): jnp.dot(coefficient, up_basis[levels - 1], preferred_element_type=F32)  2.7 us

profile of v2, /device:TPU:0, one launch (start us, length us, event | category | flops | bytes accessed | tf_op | source)
XLA Modules:
  0.0 60.8 jit_solution(15084738630998963104)
XLA Ops:
  0.0 58.1 %shard_map.46 = (f32[512,1024]{1,0:T(8,128)S(1)}, bf16[512,128]{1,0:T(8,128)(2,1)S(1)}) custom-call(bf16[512,1024]{1,0:T(8,128)(2,1)} %rhs_hbm.1, bf16[1,1024,1024]{2,1,0:T(8,128)(2,1)} %leaf_hbm.1, bf16[5,128,1024]{2,1,0:T(8,128)(2,1)} %up_hbm.1, bf16[5,256,1024]{2,1,0:T(8,128)(2,1)} %proj_hbm.1), custom_call_target="tpu_custom_call" | custom-call | tf_op jit(solution)/shard_map/pallas_call | solution.py:489
  58.1 2.7 %convolution_subtract_fusion = f32[512,1024]{1,0:T(8,128)} fusion(f32[512,1024]{1,0:T(8,128)S(1)} %get-tuple-element.7, bf16[512,128]{1,0:T(8,128)(2,1)S(1)} %get-tuple-element.8, bf16[5,128,1024]{2,1,0:T(8,128)(2,1)} %up_hbm.1), kind=kOutput, calls=%fused_computation | convolution fusion | flops 134742016 | bytes 4587520 | tf_op jit(solution)/shard_map/dot_general | solution.py:518

commit v3 on v2

--- a/solution.py
+++ b/solution.py
@@ -7,7 +7,7 @@
 from jax.experimental.pallas import tpu as pltpu
 from jax.sharding import PartitionSpec as P
 
-CHUNKS = 2
+CHUNKS = 4
 SUBLANES = 8
 F32 = jnp.float32
 BF16 = jnp.bfloat16
@@ -146,7 +146,12 @@
             entry["early"] = top == bits_x
             one, two = [own] + parts, parts
             if entry["early"]:
-                two = [functools.partial(space.reduce, bits=[top], block=top)] + parts
+                nested = [b for g in reversed(pairs(low)) for b in g]
+                direct = [functools.partial(space.reduce, bits=nested, split=nested)]
+                two = [
+                    functools.partial(space.reduce, bits=[top], block=top),
+                    functools.partial(space.reduce, bits=[height], half=height),
+                ] + (direct if len(low) <= 3 else parts)
             entry["one"], src, shape = space.chain(first, shape, one)
             entry["owned"], n = src, shape[2]
             makers = [functools.partial(space.gather, split=g) for g in reversed(pairs(low))]
@@ -191,7 +196,7 @@
     return sums, space
 
 
-def kernel(dims, plan, tables, sums, counts, rhs_hbm, leaf_hbm, up_hbm, proj_hbm, state, last_ref, *scratch):
+def kernel(dims, plan, tables, sums, counts, rhs_hbm, leaf_hbm, up_hbm, proj_hbm, state, last_ref, last_up, *scratch):
     bits_x, bits_y, levels, chunks, rows, rank = dims
     rhs, leaf, up, proj, rounded, coef, mix, mix_sum = scratch[:8]
     in_sems, send_sems, recv_sems, sum_send, sum_recv = scratch[8:13]
@@ -210,6 +215,7 @@
         loads["proj", level] = pltpu.make_async_copy(proj_hbm.at[level], proj.at[level], in_sems.at[2 + 2 * level])
         if level < levels - 1:
             loads["up", level] = pltpu.make_async_copy(up_hbm.at[level], up.at[level], in_sems.at[3 + 2 * level])
+    loads["last_up"] = pltpu.make_async_copy(up_hbm.at[levels - 1], last_up, in_sems.at[1 + 2 * levels])
     for load in loads.values():
         load.start()
 
@@ -357,7 +363,9 @@
                 for work in later:
                     work()
                 later = []
-                for i in range(max(len(one), len(two))):
+                ahead = len(two) if not entry["early"] else min(len(two), len(one)) - 1
+                at = 0
+                for i in range(max(len(one), ahead)):
                     yield
                     if i < len(one):
                         first()
@@ -365,10 +373,11 @@
                             first = begin(one[i + 1])
                         else:
                             fetch = begin(entry["gather_one"][0])
-                    if i < len(two):
+                    if at < ahead:
                         second()
-                        if i + 1 < len(two):
-                            second = begin(two[i + 1])
+                        at += 1
+                        if at < len(two):
+                            second = begin(two[at])
                 owned, joined, base = bufs[entry["owned"]], bufs[entry["joined"]], bufs[entry["partial"]]
                 n = owned.shape[2]
                 complete(height)
@@ -378,13 +387,20 @@
                     for block in range(2):
                         part = delta[block * n : (block + 1) * n, half * rank : (half + 1) * rank]
                         if entry["early"]:
-                            mine = ((pos >> height - 1) & 1) == block
-                            joined[half, block] = jnp.where(mine, base[half, 0], 0.0) - part
+                            joined[half, block] = -part
                         else:
                             joined[half, block] = base[half, block] - part
                 finish = begin(entry["last"])
                 yield
+                while at < len(two):
+                    second()
+                    at += 1
+                    if at < len(two):
+                        second = begin(two[at])
                 finish()
+                if entry["early"]:
+                    end = bufs[entry["last"].dst]
+                    end[...] = end[...] + base[...]
                 finish = begin(entry["gather_two"][0])
                 fetch()
                 for step in entry["gather_one"][1:]:
@@ -476,6 +492,19 @@
         loads.pop(key).wait()
 
 
+def finish_kernel(parts, state, coef, up, out_hbm, value, sems):
+    rows = state.shape[0] // parts
+    copies = []
+    for part in range(parts):
+        span = slice(part * rows, (part + 1) * rows)
+        value[span, :] = state[span, :] - jnp.dot(coef[span, :], up[...], preferred_element_type=F32)
+        copy = pltpu.make_async_copy(value.at[span], out_hbm.at[span], sems.at[part])
+        copy.start()
+        copies.append(copy)
+    for copy in copies:
+        copy.wait()
+
+
 def shards(rhs, leaf_inverse, up_basis, projection):
     bits_x = lax.axis_size("gx").bit_length() - 1
     bits_y = lax.axis_size("gy").bit_length() - 1
@@ -486,14 +515,15 @@
     dims = (bits_x, bits_y, levels, CHUNKS, rows, rank)
     hbm_spec = pl.BlockSpec(memory_space=pltpu.MemorySpace.HBM)
     vmem_spec = pl.BlockSpec(memory_space=pltpu.VMEM)
-    state, coefficient = pl.pallas_call(
+    state, coefficient, last_up = pl.pallas_call(
         functools.partial(kernel, dims, plan, tables, sums, (len(space.shapes),)),
         out_shape=(
             jax.ShapeDtypeStruct((rhs.shape[0], points), F32),
             jax.ShapeDtypeStruct((rhs.shape[0], rank), BF16),
+            jax.ShapeDtypeStruct((rank, points), BF16),
         ),
         in_specs=[hbm_spec] * 4,
-        out_specs=(vmem_spec, vmem_spec),
+        out_specs=(vmem_spec, vmem_spec, vmem_spec),
         scratch_shapes=[
             pltpu.VMEM(rhs.shape, BF16),
             pltpu.VMEM(leaf_inverse.shape[1:], BF16),
@@ -515,7 +545,15 @@
             collective_id=0, has_side_effects=True, vmem_limit_bytes=44 * 2**20
         ),
     )(*[pltpu.with_memory_space_constraint(x, pltpu.MemorySpace.HBM) for x in (rhs, leaf_inverse, up_basis, projection)])
-    return state - jnp.dot(coefficient, up_basis[levels - 1], preferred_element_type=F32)
+    parts = 4
+    return pl.pallas_call(
+        functools.partial(finish_kernel, parts),
+        out_shape=jax.ShapeDtypeStruct(state.shape, F32),
+        in_specs=[vmem_spec] * 3,
+        out_specs=pl.BlockSpec(memory_space=pl.ANY),
+        scratch_shapes=[pltpu.VMEM(state.shape, F32), pltpu.SemaphoreType.DMA((parts,))],
+        compiler_params=pltpu.CompilerParams(vmem_limit_bytes=8 * 2**20),
+    )(state, coefficient, last_up)
 
 
 def solution(mesh):

time: 61 us -> 59.3 us (0.972)
  matrix products: 2.7 us -> 0 us
  Pallas kernels: 58.1 us -> 59 us
    dot_general x1 -> x0, matrix products: 2.7 us -> none  [shards(): jnp.dot(coefficient, up_basis[levels - 1], preferred_element_type=F32)]
    pallas_call x0 -> x1, Pallas kernels: none -> 1.57 us  [shards(): pl.pallas_call(functools.partial(finish_kernel, parts), out_shape=jax.Sha...]
    pallas_call x1, Pallas kernels: 58.1 us -> 57.5 us  [shards(): pl.pallas_call(functools.partial(kernel, dims, plan, tables, sums, (len(s...]
where the time goes in v3:
time: 59.3 us; the launch traced here: 59 us
  Pallas kernels  59 us (99%)
    pallas_call x1, Pallas kernels, shards(): pl.pallas_call(functools.partial(kernel, dims, plan, tables, sums, (len(s...  57.5 us
    pallas_call x1, Pallas kernels, shards(): pl.pallas_call(functools.partial(finish_kernel, parts), out_shape=jax.Sha...  1.57 us

profile of v3, /device:TPU:0, one launch (start us, length us, event | category | flops | bytes accessed | tf_op | source)
XLA Modules:
  0.0 59.0 jit_solution(8318389824096743740)
XLA Ops:
  0.0 57.5 %shard_map.46 = (f32[512,1024]{1,0:T(8,128)S(1)}, bf16[512,128]{1,0:T(8,128)(2,1)S(1)}, bf16[128,1024]{1,0:T(8,128)(2,1)S(1)}) custom-call(bf16[512,1024]{1,0:T(8,128)(2,1)} %rhs_hbm.1, bf16[1,1024,1024]{2,1,0:T(8,128)(2,1)} %leaf_hbm.1, bf16[5,128,1024]{2,1,0:T(8,128)(2,1)} %up_hbm.1, bf16[5,256,1024]{2,1,0:T(8,128)(2,1)} %proj_hbm.1), custom_call_target="tpu_custom_call" | custom-call | tf_op jit(solution)/shard_map/pallas_call | solution.py:518
  57.5 1.6 %shard_map.47 = f32[512,1024]{1,0:T(8,128)} custom-call(f32[512,1024]{1,0:T(8,128)S(1)} %get-tuple-element.8.state, bf16[512,128]{1,0:T(8,128)(2,1)S(1)} %get-tuple-element.9.coef, bf16[128,1024]{1,0:T(8,128)(2,1)S(1)} %get-tuple-element.10.up), custom_call_target="tpu_custom_call" | custom-call | tf_op jit(solution)/shard_map/pallas_call | solution.py:549

commit v4 on v3

--- a/solution.py
+++ b/solution.py
@@ -239,7 +239,7 @@
     for mask in sorted(greeted):
         pl.semaphore_signal(barrier, inc=1, device_id=device(mask), device_id_type=MESH)
 
-    sent = []
+    sent, idle = [], []
 
     def start(step, bufs, send, recv):
         src, dst = bufs[step.src], bufs[step.dst]
@@ -344,8 +344,7 @@
                 height = group[0]
                 for step in entry["reduce"] + entry["gather"]:
                     finish = begin(step)
-                    for work in later:
-                        work()
+                    idle.extend(later)
                     later = []
                     yield
                     if height == 1 and step is entry["reduce"][0]:
@@ -360,8 +359,7 @@
                 height = group[0]
                 one, two = entry["one"], entry["two"]
                 first, second = begin(one[0]), begin(two[0])
-                for work in later:
-                    work()
+                idle.extend(later)
                 later = []
                 ahead = len(two) if not entry["early"] else min(len(two), len(one)) - 1
                 at = 0
@@ -468,7 +466,7 @@
                     if (low, high) == (height, height + 1):
                         for half in range(2):
                             sum_bufs[src][half, 0] = value[:, half * rank : (half + 1) * rank]
-        for height, _, _, _ in sums[1:]:
+        for height, _, _, _ in sums:
             advance(height)
         yield
         for _ in range(max([0] + [len(steps) + 1 for _, _, steps, _ in sums])):
@@ -486,6 +484,8 @@
             except StopIteration:
                 pass
         flows = left
+        while idle:
+            idle.pop(0)()
     for copy in sent:
         copy.wait_send()
     for key in list(loads):
@@ -545,7 +545,7 @@
             collective_id=0, has_side_effects=True, vmem_limit_bytes=44 * 2**20
         ),
     )(*[pltpu.with_memory_space_constraint(x, pltpu.MemorySpace.HBM) for x in (rhs, leaf_inverse, up_basis, projection)])
-    parts = 4
+    parts = 8
     return pl.pallas_call(
         functools.partial(finish_kernel, parts),
         out_shape=jax.ShapeDtypeStruct(state.shape, F32),

time: 59.3 us -> 59.1 us (level)
  no operation moved by 1% of the time
where the time goes in v4:
time: 59.1 us; the launch traced here: 58.9 us
  Pallas kernels  58.9 us (100%)
    pallas_call x1, Pallas kernels, shards(): pl.pallas_call(functools.partial(kernel, dims, plan, tables, sums, (len(s...  57.3 us
    pallas_call x1, Pallas kernels, shards(): pl.pallas_call(functools.partial(finish_kernel, parts), out_shape=jax.Sha...  1.57 us

profile of v4, /device:TPU:0, one launch (start us, length us, event | category | flops | bytes accessed | tf_op | source)
XLA Modules:
  0.0 58.9 jit_solution(11754625176877510633)
XLA Ops:
  0.0 57.3 %shard_map.46 = (f32[512,1024]{1,0:T(8,128)S(1)}, bf16[512,128]{1,0:T(8,128)(2,1)S(1)}, bf16[128,1024]{1,0:T(8,128)(2,1)S(1)}) custom-call(bf16[512,1024]{1,0:T(8,128)(2,1)} %rhs_hbm.1, bf16[1,1024,1024]{2,1,0:T(8,128)(2,1)} %leaf_hbm.1, bf16[5,128,1024]{2,1,0:T(8,128)(2,1)} %up_hbm.1, bf16[5,256,1024]{2,1,0:T(8,128)(2,1)} %proj_hbm.1), custom_call_target="tpu_custom_call" | custom-call | tf_op jit(solution)/shard_map/pallas_call | solution.py:518
  57.3 1.6 %shard_map.47 = f32[512,1024]{1,0:T(8,128)} custom-call(f32[512,1024]{1,0:T(8,128)S(1)} %get-tuple-element.8.state, bf16[512,128]{1,0:T(8,128)(2,1)S(1)} %get-tuple-element.9.coef, bf16[128,1024]{1,0:T(8,128)(2,1)S(1)} %get-tuple-element.10.up), custom_call_target="tpu_custom_call" | custom-call | tf_op jit(solution)/shard_map/pallas_call | solution.py:549

commit v5 on v4

--- a/solution.py
+++ b/solution.py
@@ -348,8 +348,9 @@
                     later = []
                     yield
                     if height == 1 and step is entry["reduce"][0]:
-                        for other in range(2, levels + 1):
+                        for other in after:
                             project(other)
+                        idle.extend(functools.partial(project, other) for other in beyond)
                     finish()
                 keep(height, bufs[entry["result"]])
                 if height < levels:

time: 59.1 us -> 59.1 us (level)
  no operation moved by 1% of the time
where the time goes in v5:
time: 59.1 us; the launch traced here: 58.9 us
  Pallas kernels  58.9 us (100%)
    pallas_call x1, Pallas kernels, shards(): pl.pallas_call(functools.partial(kernel, dims, plan, tables, sums, (len(s...  57.3 us
    pallas_call x1, Pallas kernels, shards(): pl.pallas_call(functools.partial(finish_kernel, parts), out_shape=jax.Sha...  1.57 us

profile of v5, /device:TPU:0, one launch (start us, length us, event | category | flops | bytes accessed | tf_op | source)
XLA Modules:
  0.0 58.9 jit_solution(17909528084165315591)
XLA Ops:
  0.0 57.3 %shard_map.46 = (f32[512,1024]{1,0:T(8,128)S(1)}, bf16[512,128]{1,0:T(8,128)(2,1)S(1)}, bf16[128,1024]{1,0:T(8,128)(2,1)S(1)}) custom-call(bf16[512,1024]{1,0:T(8,128)(2,1)} %rhs_hbm.1, bf16[1,1024,1024]{2,1,0:T(8,128)(2,1)} %leaf_hbm.1, bf16[5,128,1024]{2,1,0:T(8,128)(2,1)} %up_hbm.1, bf16[5,256,1024]{2,1,0:T(8,128)(2,1)} %proj_hbm.1), custom_call_target="tpu_custom_call" | custom-call | tf_op jit(solution)/shard_map/pallas_call | solution.py:519
  57.3 1.6 %shard_map.47 = f32[512,1024]{1,0:T(8,128)} custom-call(f32[512,1024]{1,0:T(8,128)S(1)} %get-tuple-element.8.state, bf16[512,128]{1,0:T(8,128)(2,1)S(1)} %get-tuple-element.9.coef, bf16[128,1024]{1,0:T(8,128)(2,1)S(1)} %get-tuple-element.10.up), custom_call_target="tpu_custom_call" | custom-call | tf_op jit(solution)/shard_map/pallas_call | solution.py:550
